TPU v7x, 32 devices: a whole 2x2x4 slice. The times are simulated.
32 devices in a mesh: blk: 16 (over z, y, core), mp: 2 (over x).
Axes of the slice: x: 2, y: 2, z: 4, core: 2. Of those that a mesh axis runs over, the one named last changes fastest.
Arguments:
- params: bfloat16 [16, 1024, 4096], P('blk', None, 'mp'), may hold values from -0.09375 to 0.09375
- hidden: bfloat16 [16, 384, 4096], P('blk', None, 'mp'), may hold values from -6 to 6
- targets: bfloat16 [16, 384, 1024], P('blk', None, 'mp'), may hold values from -6 to 6
Outputs:
- params_out: bfloat16 [16, 1024, 4096], P('blk', None, 'mp')
- errors: float32 [2], replicated
All inputs are finite; a program needn't handle non-finite values.
Results may differ from a plain program's by a relative error of at most 0.0085.
Values may be sent and summed in bfloat16 or wider, within the bound.
A program may use at most 128 MiB of HBM per device.

v0:
```python
import jax
import jax.numpy as jnp
from jax import lax
from jax.sharding import PartitionSpec as P

ITERS = 2


mix_third = 1.0 / 3.0
step_size = 0.1


def from_behind(block, axis, distance):
    devices = range(lax.axis_size(axis))
    route = [((i - distance) % len(devices), i) for i in devices]
    return lax.ppermute(block, axis, route)


def send_tracker(track):
    track_left = from_behind(track, "blk", 1)
    track_right = from_behind(track, "blk", -1)
    return (track_left, track_right)


def on_device(params, hidden, targets):
    state = params[0]
    feats = hidden[0]
    targ_local = targets[0]
    tokens = feats.shape[0]
    hidden_total = state.shape[1] * lax.axis_size("mp")
    replicas = lax.axis_size("blk")

    def gradient(weight):
        partial_value = lax.dot_general(
            feats, weight, (((1,), (1,)), ((), ())), preferred_element_type=jnp.float32
        )
        share = lax.psum_scatter(partial_value, "mp", scatter_dimension=1, tiled=True)
        resid_local = (share - targ_local.astype(jnp.float32)).astype(jnp.bfloat16)
        resid = lax.all_gather(resid_local, "mp", axis=1, tiled=True)
        grad = lax.dot_general(
            resid, feats, (((0,), (0,)), ((), ())), preferred_element_type=jnp.float32
        )
        return grad / tokens

    older = gradient(state)
    fresh = older
    track = older.astype(jnp.bfloat16)
    track_left, track_right = send_tracker(track)
    err_list = []
    for step in range(ITERS):
        state_left = from_behind(state, "blk", 1)
        state_right = from_behind(state, "blk", -1)
        if step > 0:
            track_mix = (
                track_left.astype(jnp.float32)
                + track.astype(jnp.float32)
                + track_right.astype(jnp.float32)
            ) * mix_third
            track = (track_mix + fresh - older).astype(jnp.bfloat16)
            older = fresh
        own_state = state.astype(jnp.float32)
        diff = own_state - state_right.astype(jnp.float32)
        local_err = jnp.sum(diff * diff) / (hidden_total * replicas)
        err_list.append(lax.psum(local_err, ("blk", "mp")))
        blended = (
            state_left.astype(jnp.float32) + own_state + state_right.astype(jnp.float32)
        ) * mix_third
        new_state = (blended - step_size * track.astype(jnp.float32)).astype(jnp.bfloat16)
        if step < ITERS - 1:
            fresh = gradient(new_state)
        state = new_state
    errors = jnp.stack(err_list)
    return (state[None], errors)


def solution(mesh):
    placed = (P("blk", None, "mp"), P("blk", None, "mp"), P("blk", None, "mp"))
    return jax.shard_map(
        on_device,
        mesh=mesh,
        in_specs=placed,
        out_specs=(P("blk", None, "mp"), P()),
        check_vma=False,
    )
```

profile of v0, /device:TPU:0, one launch (start us, length us, event | category | flops | bytes accessed | tf_op | source)
XLA Modules:
  0.0 399.6 jit_solution(2911547974438466488)
XLA Ops:
  7.2 0.0 copy-start
  7.2 0.0 reduce-scatter.3.cloned.1.call-start
  7.2 0.0 copy-start.1
  7.2 5.5 %collective-permute-start.1 = (bf16[1024,2048]{1,0:T(8,128)(2,1)}, bf16[1024,2048]{1,0:T(8,128)(2,1)}, u32[]{:S(2)}, u32[]{:S(2)}) collective-permute-start(bf16[1024,2048]{1,0:T(8,128)(2,1)} %bitcast.31), channel_id=1, source_target_pairs={{2,0},{4,2},{6,4},{8,6},{10,8},{12,10},{14,12},{16,14},{18,16},{20... | collective-permute-start | bytes 12582920 | tf_op jit(solution)/shard_map/ppermute | solution.py:16
  12.8 0.0 collective-permute-start
  12.8 0.0 copy-done
  12.8 5.2 %fusion.21 = f32[384,1024]{1,0:T(8,128)} fusion(bf16[1,384,2048]{2,1,0:T(8,128)(2,1)S(1)} %copy-done, bf16[1,1024,2048]{2,1,0:T(8,128)(2,1)} %param.3), kind=kOutput, calls=%fused_computation.30 | convolution fusion | flops 1610612736 | bytes 7340032 | tf_op jit(solution)/shard_map/dot_general | solution.py:34
  17.9 0.0 reduce-scatter.3.cloned.1.call-update
  18.0 0.0 reduce-scatter.5.cloned.1.call-start
  18.0 27.4 %reduce-scatter.3.cloned.1.call-done = f32[384,512]{1,0:T(8,128)} async-done(((f32[384,1024]{1,0:T(8,128)}), f32[384,512]{1,0:T(8,128)}) %reduce-scatter.3.cloned.1.call-update) | async-done | bytes 786448 | tf_op jit(solution)/shard_map/reduce_scatter | solution.py:37
  45.4 0.0 copy-done.1
  45.4 1.3 fusion.26
  46.7 11.4 %all_gather.6 = bf16[384,1024]{1,0:T(8,128)(2,1)S(1)} all-gather(bf16[384,512]{1,0:T(8,128)(2,1)S(1)} %fusion.26), channel_id=1, replica_groups=mesh['blk'=16,'mp'=2] {'mp'}, dimensions={1}, use_global_device_ids=true | all-gather | bytes 1179648 | tf_op jit(solution)/shard_map/all_gather | solution.py:39
  58.1 1.0 collective-permute-done.1
  59.1 4.7 %collective-permute-done = bf16[1024,2048]{1,0:T(8,128)(2,1)} collective-permute-done((bf16[1024,2048]{1,0:T(8,128)(2,1)}, bf16[1024,2048]{1,0:T(8,128)(2,1)}, u32[]{:S(2)}, u32[]{:S(2)}) %collective-permute-start) | collective-permute-done | bytes 4194336 | tf_op jit(solution)/shard_map/ppermute | solution.py:16
  63.8 12.3 %fusion.4 = (f32[]{:T(128)}, bf16[1024,2048]{1,0:T(8,128)(2,1)}, bf16[1024,2048]{1,0:T(8,128)(2,1)}, f32[1024,2048]{1,0:T(8,128)}) fusion(bf16[1024,2048]{1,0:T(8,128)(2,1)} %collective-permute-done.1, bf16[1,1024,2048]{2,1,0:T(8,128)(2,1)} %param.3, bf16[1024,2048]{1,0:T(8,128)(2,1)} %collective-permute-done, bf16[384,1024]{1,0:T(8,128)(2,1)S(1)} %all_gather.6, ...), kind=kOutput, calls=%fused_computation.12 | convolution fusion | flops 1642070016 | bytes 31719428 | tf_op jit(solution)/shard_map/dot_general | solution.py:40
  76.1 0.0 collective-permute-start.3
  76.1 5.2 %fusion.23 = f32[384,1024]{1,0:T(8,128)} fusion(bf16[1024,2048]{1,0:T(8,128)(2,1)} %get-tuple-element.5, bf16[1,384,2048]{2,1,0:T(8,128)(2,1)S(1)} %copy-done), kind=kOutput, calls=%fused_computation.32 | convolution fusion | flops 1610612736 | bytes 7340032 | tf_op jit(solution)/shard_map/dot_general | solution.py:34
  81.4 0.0 reduce-scatter.5.cloned.1.call-update
  81.4 82.3 %collective-permute-start.4 = (bf16[1024,2048]{1,0:T(8,128)(2,1)}, bf16[1024,2048]{1,0:T(8,128)(2,1)}, u32[]{:S(2)}, u32[]{:S(2)}) collective-permute-start(bf16[1024,2048]{1,0:T(8,128)(2,1)} %get-tuple-element.6), channel_id=1, source_target_pairs={{30,0},{0,2},{2,4},{4,6},{6,8},{8,10},{10,12},{12,14},{14,16},{16,... | collective-permute-start | bytes 12582920 | tf_op jit(solution)/shard_map/ppermute | solution.py:16
  163.7 5.6 %collective-permute-start.5 = (bf16[1024,2048]{1,0:T(8,128)(2,1)}, bf16[1024,2048]{1,0:T(8,128)(2,1)}, u32[]{:S(2)}, u32[]{:S(2)}) collective-permute-start(bf16[1024,2048]{1,0:T(8,128)(2,1)} %get-tuple-element.6), channel_id=1, source_target_pairs={{2,0},{4,2},{6,4},{8,6},{10,8},{12,10},{14,12},{16,14},{18,16},{20... | collective-permute-start | bytes 12582920 | tf_op jit(solution)/shard_map/ppermute | solution.py:16
  169.3 0.0 collective-permute-start.2
  170.0 22.3 %reduce-scatter.5.cloned.1.call-done = f32[384,512]{1,0:T(8,128)} async-done(((f32[384,1024]{1,0:T(8,128)}), f32[384,512]{1,0:T(8,128)}) %reduce-scatter.5.cloned.1.call-update) | async-done | bytes 786448 | tf_op jit(solution)/shard_map/reduce_scatter | solution.py:37
  192.2 1.3 fusion.27
  193.5 11.3 %all_gather.7 = bf16[384,1024]{1,0:T(8,128)(2,1)S(1)} all-gather(bf16[384,512]{1,0:T(8,128)(2,1)S(1)} %fusion.27), channel_id=1, replica_groups=mesh['blk'=16,'mp'=2] {'mp'}, dimensions={1}, use_global_device_ids=true | all-gather | bytes 1179648 | tf_op jit(solution)/shard_map/all_gather | solution.py:39
  204.8 0.0 collective-permute-done.3
  204.8 6.3 %fusion.14 = f32[]{:T(128)} fusion(bf16[1024,2048]{1,0:T(8,128)(2,1)} %collective-permute-done.3, bf16[1024,2048]{1,0:T(8,128)(2,1)} %get-tuple-element.5), kind=kLoop, calls=%fused_computation.22 | loop fusion | flops 10485759 | bytes 8388612 | tf_op jit(solution)/shard_map/reduce_sum | solution.py:63
  211.7 165.2 %all-reduce = (f32[1]{0:T(128)}, f32[1]{0:T(128)}) all-reduce(f32[1]{0:T(128)} %bitcast.7, f32[1]{0:T(128)} %bitcast.6), channel_id=1, replica_groups=mesh['blk'=16,'mp'=2] {'blk','mp'}, use_global_device_ids=true, to_apply=%region_5.0 | all-reduce | flops 2 | bytes 16 | tf_op jit(solution)/shard_map/psum | solution.py:64
  377.0 1.9 pad_maximum_fusion
  378.9 0.0 collective-permute-done.4
  378.9 0.0 collective-permute-done.5
  378.9 0.0 collective-permute-done.2
  378.9 13.9 %fusion.15 = bf16[1,1024,2048]{2,1,0:T(8,128)(2,1)} fusion(bf16[1024,2048]{1,0:T(8,128)(2,1)} %collective-permute-done.3, bf16[1024,2048]{1,0:T(8,128)(2,1)} %get-tuple-element.5, bf16[1024,2048]{1,0:T(8,128)(2,1)} %collective-permute-done.2, f32[1024,2048]{1,0:T(8,128)} %get-tuple-element.7, bf16[384,1024]{1,0:T(8,128)(2,1)S(1)} %all_gather.7, ...), kind=kOutput, calls=%fused_computation.24 | convolution fusion | flops 1656750080 | bytes 35913728 | tf_op jit(solution)/shard_map/dot_general | solution.py:40
Async XLA Ops:
  7.2 5.6 %copy-start = (bf16[1,384,2048]{2,1,0:T(8,128)(2,1)S(1)}, bf16[1,384,2048]{2,1,0:T(8,128)(2,1)}, u32[]{:S(2)}) copy-start(bf16[1,384,2048]{2,1,0:T(8,128)(2,1)} %param.4) | copy-start | bytes 4718596
  7.2 38.3 %reduce-scatter.3.cloned.1.call-start = ((), (), s32[]{:S(2)}) async-start(), calls=%async_computation.2 | async-start | bytes 2359296 | tf_op jit(solution)/shard_map/reduce_scatter | solution.py:37
  7.2 38.2 %copy-start.1 = (bf16[1,384,512]{2,1,0:T(8,128)(2,1)S(1)}, bf16[1,384,512]{2,1,0:T(8,128)(2,1)}, u32[]{:S(2)}) copy-start(bf16[1,384,512]{2,1,0:T(8,128)(2,1)} %param.5) | copy-start | bytes 1179652
  7.2 51.9 %collective-permute-start.1 = (bf16[1024,2048]{1,0:T(8,128)(2,1)}, bf16[1024,2048]{1,0:T(8,128)(2,1)}, u32[]{:S(2)}, u32[]{:S(2)}) collective-permute-start(bf16[1024,2048]{1,0:T(8,128)(2,1)} %bitcast.31), channel_id=1, source_target_pairs={{2,0},{4,2},{6,4},{8,6},{10,8},{12,10},{14,12},{16,14},{18,16},{20... | collective-permute-start | bytes 12582920 | tf_op jit(solution)/shard_map/ppermute | solution.py:16
  12.8 51.0 %collective-permute-start = (bf16[1024,2048]{1,0:T(8,128)(2,1)}, bf16[1024,2048]{1,0:T(8,128)(2,1)}, u32[]{:S(2)}, u32[]{:S(2)}) collective-permute-start(bf16[1024,2048]{1,0:T(8,128)(2,1)} %bitcast.32), channel_id=1, source_target_pairs={{30,0},{0,2},{2,4},{4,6},{6,8},{8,10},{10,12},{12,14},{14,16},{16,... | collective-permute-start | bytes 12582920 | tf_op jit(solution)/shard_map/ppermute | solution.py:16
  18.0 174.3 %reduce-scatter.5.cloned.1.call-start = ((), (), s32[]{:S(2)}) async-start(), calls=%async_computation.3 | async-start | bytes 2359296 | tf_op jit(solution)/shard_map/reduce_scatter | solution.py:37
  76.1 128.7 %collective-permute-start.3 = (bf16[1024,2048]{1,0:T(8,128)(2,1)}, bf16[1024,2048]{1,0:T(8,128)(2,1)}, u32[]{:S(2)}, u32[]{:S(2)}) collective-permute-start(bf16[1024,2048]{1,0:T(8,128)(2,1)} %get-tuple-element.5), channel_id=1, source_target_pairs={{2,0},{4,2},{6,4},{8,6},{10,8},{12,10},{14,12},{16,14},{18,16},{20... | collective-permute-start | bytes 12582920 | tf_op jit(solution)/shard_map/ppermute | solution.py:16
  81.4 297.5 %collective-permute-start.4 = (bf16[1024,2048]{1,0:T(8,128)(2,1)}, bf16[1024,2048]{1,0:T(8,128)(2,1)}, u32[]{:S(2)}, u32[]{:S(2)}) collective-permute-start(bf16[1024,2048]{1,0:T(8,128)(2,1)} %get-tuple-element.6), channel_id=1, source_target_pairs={{30,0},{0,2},{2,4},{4,6},{6,8},{8,10},{10,12},{12,14},{14,16},{16,... | collective-permute-start | bytes 12582920 | tf_op jit(solution)/shard_map/ppermute | solution.py:16
  163.7 215.1 %collective-permute-start.5 = (bf16[1024,2048]{1,0:T(8,128)(2,1)}, bf16[1024,2048]{1,0:T(8,128)(2,1)}, u32[]{:S(2)}, u32[]{:S(2)}) collective-permute-start(bf16[1024,2048]{1,0:T(8,128)(2,1)} %get-tuple-element.6), channel_id=1, source_target_pairs={{2,0},{4,2},{6,4},{8,6},{10,8},{12,10},{14,12},{16,14},{18,16},{20... | collective-permute-start | bytes 12582920 | tf_op jit(solution)/shard_map/ppermute | solution.py:16
  169.3 209.6 %collective-permute-start.2 = (bf16[1024,2048]{1,0:T(8,128)(2,1)}, bf16[1024,2048]{1,0:T(8,128)(2,1)}, u32[]{:S(2)}, u32[]{:S(2)}) collective-permute-start(bf16[1024,2048]{1,0:T(8,128)(2,1)} %get-tuple-element.5), channel_id=1, source_target_pairs={{30,0},{0,2},{2,4},{4,6},{6,8},{8,10},{10,12},{12,14},{14,16},{16,... | collective-permute-start | bytes 12582920 | tf_op jit(solution)/shard_map/ppermute | solution.py:16
Sparse Core Ops, SparseCore 0:
  18.1 27.3 reduce-scatter.2
  81.5 110.6 reduce-scatter.4
where the time goes:
time: 400 us
  blocking collectives  188 us (47%)
  starting transfers between devices  93.5 us (23%)
  waiting for transfers between devices  55.5 us (14%)
  matrix products  36.7 us (9%)
  between operations  15.4 us (4%)
  other arithmetic  10.7 us (3%)
    psum x1, blocking collectives, on_device(): err_list.append(lax.psum(local_err, ('blk', 'mp')))  165 us
    ppermute x6, starting transfers between devices, from_behind(): return lax.ppermute(block, axis, route)  93.4 us
    reduce_scatter x2, waiting for transfers between devices, gradient(): lax.psum_scatter(partial_value, 'mp', scatter_dimension=1, tiled=True)  49.7 us
    dot_general x2, matrix products, gradient(): lax.dot_general(resid, feats, (((0,), (0,)), ((), ())), preferred_element...  26.3 us
    all_gather x2, blocking collectives, gradient(): resid = lax.all_gather(resid_local, 'mp', axis=1, tiled=True)  22.7 us
    dot_general x2, matrix products, gradient(): lax.dot_general(feats, weight, (((1,), (1,)), ((), ())), preferred_elemen...  10.4 us
  transfers between devices with their start and end apart: 8, of which 4 were waited for; matrix products, arithmetic and copies ran while one was open for 5% of the time, Pallas kernels for 0%

commit v1 on v0

v1 whole, which is shorter than its diff:
```python
import functools

import jax
import jax.numpy as jnp
from jax import lax
from jax.experimental import pallas as pl
from jax.experimental.pallas import tpu as pltpu
from jax.sharding import PartitionSpec as P

MESH = pl.DeviceIdType.MESH
CHUNKS = 4
COLS = 4
mix_third = 1.0 / 3.0
step_size = 0.1
F32 = jnp.float32
BF16 = jnp.bfloat16


def dot_nt(a, b):
    return lax.dot_general(a, b, (((1,), (1,)), ((), ())), preferred_element_type=F32)


def dot_nn(a, b):
    return lax.dot_general(a, b, (((1,), (0,)), ((), ())), preferred_element_type=F32)


def kernel(n, x, h, t, out, err, far, near, hn, rt, rt2, rn, ps, pr, acc, sems, one):
    d, wide = x.shape
    tokens = h.shape[0]
    half = t.shape[0]
    rows = d // CHUNKS
    cw = wide // COLS
    me = lax.axis_index("blk")
    mp = lax.axis_index("mp")
    core = lax.rem(me, 2)
    par = lax.rem(me // 2, 2)
    sib = me + 1 - 2 * core
    partner = me + 2 - 4 * par
    fwd_to = lax.rem(me + n + 4 - 8 * par, n)
    fwd_from = lax.rem(me + n - 4 + 8 * par, n)
    cross = lax.rem(me + n + 2 * core - 1, n)

    barrier = pltpu.get_barrier_semaphore()
    peers = [(sib, mp), (partner, mp), (fwd_to, mp), (fwd_from, mp), (cross, mp), (me, 1 - mp)]
    for peer in peers:
        pl.semaphore_signal(barrier, inc=1, device_id=peer, device_id_type=MESH)
    pl.semaphore_wait(barrier, len(peers))

    def rs(k):
        return pl.ds(k * rows, rows)

    def copy(src, dst, kind, k, dev):
        return pltpu.make_async_remote_copy(
            src_ref=src, dst_ref=dst, send_sem=sems.at[0, kind, k], recv_sem=sems.at[1, kind, k],
            device_id=dev, device_id_type=MESH)

    def c_own(k):
        return copy(x.at[rs(k)], far.at[par, rs(k)], 0, k, (partner, mp))

    def c_fwd(k):
        return copy(far.at[1 - par, rs(k)], far.at[par, rs(k)], 1, k, (fwd_to, mp))

    def c_cross(k):
        return copy(far.at[1 - core, rs(k)], near.at[1 - core, rs(k)], 2, k, (sib, mp))

    def c_rsib(k):
        return copy(rt.at[rs(k)], rn.at[core, rs(k)], 3, k, (sib, mp))

    def c_rcross(k):
        return copy(rt.at[rs(k)], rn.at[1 - core, rs(k)], 4, k, (cross, mp))

    def c_part(it, k):
        return copy(ps.at[it, rs(k)], pr.at[it, rs(k)], 5 + it, k, (me, 1 - mp))

    def c_hcross(j):
        cs = pl.ds(j * cw, cw)
        return copy(h.at[:, cs], hn.at[1 - core, :, cs], 7, j, (cross, mp))

    c_sib = pltpu.make_async_remote_copy(
        src_ref=x, dst_ref=near.at[core], send_sem=one.at[0, 0], recv_sem=one.at[1, 0],
        device_id=(sib, mp), device_id_type=MESH)
    c_hsib = pltpu.make_async_remote_copy(
        src_ref=h, dst_ref=hn.at[core], send_sem=one.at[0, 1], recv_sem=one.at[1, 1],
        device_id=(sib, mp), device_id_type=MESH)

    def send_part(it, k, value):
        first = k * rows
        mine = mp == first // half
        targ = t[pl.ds(first % half, rows), :].astype(F32)
        ps[it, rs(k), :] = (value - jnp.where(mine, targ, 0.0)).astype(BF16)
        c_part(it, k).start()

    def take_part(it, k, dst):
        c_part(it, k).wait_recv()
        dst[rs(k), :] = (ps[it, rs(k), :].astype(F32) + pr[it, rs(k), :].astype(F32)).astype(BF16)

    early = CHUNKS // 2
    for k in range(early):
        c_own(k).start()
    c_sib.start()
    c_hsib.start()
    acc[...] = jnp.zeros_like(acc)
    for k in range(CHUNKS):
        send_part(0, k, dot_nt(x[rs(k), :], h[...]))
    for k in range(CHUNKS):
        take_part(0, k, rt)
        c_rcross(k).start()
        c_rsib(k).start()
    for k in range(early, CHUNKS):
        c_own(k).start()
    for j in range(COLS):
        c_hcross(j).start()
    c_sib.wait_recv()

    for s in range(CHUNKS + 2):
        if s < CHUNKS:
            c_own(s).wait_recv()
            c_fwd(s).start()
        k = s - 1
        if 0 <= k < CHUNKS:
            c_fwd(k).wait_recv()
            c_cross(k).start()
            c_cross(k).wait_recv()

            def first_step(j, _, k=k):
                cs = pl.ds(pl.multiple_of(j * cw, cw), cw)
                track = (dot_nn(rt[rs(k), :], h[:, cs]) / tokens).astype(BF16)
                own = x[rs(k), cs].astype(F32)
                blend = (near[0, rs(k), cs].astype(F32) + own + near[1, rs(k), cs].astype(F32)) * mix_third
                out[rs(k), cs] = (blend - step_size * track.astype(F32)).astype(BF16)
                return 0

            lax.fori_loop(0, COLS, first_step, 0)
            send_part(1, k, dot_nt(out[rs(k), :], h[...]))
        k = s - 2
        if 0 <= k < CHUNKS:
            take_part(1, k, rt2)

    c_hsib.wait_recv()
    for k in range(CHUNKS):
        c_rsib(k).wait_recv()
        c_rcross(k).wait_recv()

    for j in range(COLS):
        c_hcross(j).wait_recv()
        cs = pl.ds(j * cw, cw)

        def last_step(k, _, cs=cs):
            r = pl.ds(pl.multiple_of(k * rows, rows), rows)
            older = dot_nn(rt[r, :], h[:, cs]) / tokens
            fresh = dot_nn(rt2[r, :], h[:, cs]) / tokens
            below = (dot_nn(rn[0, r, :], hn[0, :, cs]) / tokens).astype(BF16).astype(F32)
            above = (dot_nn(rn[1, r, :], hn[1, :, cs]) / tokens).astype(BF16).astype(F32)
            track = older.astype(BF16).astype(F32)
            track = ((below + track + above) * mix_third + fresh - older).astype(BF16).astype(F32)
            own = x[r, cs].astype(F32)
            lo = near[0, r, cs].astype(F32)
            hi = near[1, r, cs].astype(F32)
            x_lo = (far[0, r, cs].astype(F32) + lo + own) * mix_third - step_size * below
            x_hi = (own + hi + far[1, r, cs].astype(F32)) * mix_third - step_size * above
            x_lo = x_lo.astype(BF16).astype(F32)
            x_hi = x_hi.astype(BF16).astype(F32)
            x_me = out[r, cs].astype(F32)
            diff = own - hi
            acc[0:1, :] += jnp.sum(diff * diff, axis=0, keepdims=True)
            diff = x_me - x_hi
            acc[1:2, :] += jnp.sum(diff * diff, axis=0, keepdims=True)
            out[r, cs] = ((x_lo + x_me + x_hi) * mix_third - step_size * track).astype(BF16)
            return 0

        lax.fori_loop(0, CHUNKS, last_step, 0)

    err[...] = acc[...]
    c_sib.wait_send()
    c_hsib.wait_send()
    for k in range(CHUNKS):
        for c in (c_own(k), c_fwd(k), c_cross(k), c_rsib(k), c_rcross(k), c_part(0, k), c_part(1, k)):
            c.wait_send()
    for j in range(COLS):
        c_hcross(j).wait_send()


def solution(mesh):
    n = mesh.shape["blk"]

    def on_device(params, hidden, targets):
        x, h, t = params[0], hidden[0], targets[0].T
        d, wide = x.shape
        tokens = h.shape[0]
        total = wide * mesh.shape["mp"] * n
        vmem = pl.BlockSpec(memory_space=pltpu.VMEM)
        kinds = 8
        most = max(CHUNKS, COLS)
        new, part = pl.pallas_call(
            functools.partial(kernel, n),
            out_shape=(jax.ShapeDtypeStruct((d, wide), BF16),
                       jax.ShapeDtypeStruct((2, wide // COLS), F32)),
            in_specs=[vmem] * 3,
            out_specs=(vmem, vmem),
            scratch_shapes=[
                pltpu.VMEM((2, d, wide), BF16),
                pltpu.VMEM((2, d, wide), BF16),
                pltpu.VMEM((2, tokens, wide), BF16),
                pltpu.VMEM((d, tokens), BF16),
                pltpu.VMEM((d, tokens), BF16),
                pltpu.VMEM((2, d, tokens), BF16),
                pltpu.VMEM((2, d, tokens), BF16),
                pltpu.VMEM((2, d, tokens), BF16),
                pltpu.VMEM((2, wide // COLS), F32),
                pltpu.SemaphoreType.DMA((2, kinds, most)),
                pltpu.SemaphoreType.DMA((2, 2)),
            ],
            compiler_params=pltpu.CompilerParams(
                collective_id=0, has_side_effects=True, vmem_limit_bytes=60 * 1024 * 1024),
        )(x, h, t)
        errors = lax.psum(jnp.sum(part, axis=1), ("blk", "mp")) / total
        return new[None], errors

    placed = (P("blk", None, "mp"),) * 3
    return jax.shard_map(
        on_device, mesh=mesh, in_specs=placed,
        out_specs=(P("blk", None, "mp"), P()), check_vma=False)
```

time: 400 us -> 235 us (0.59)
  Pallas kernels: 0 us -> 187 us
  blocking collectives: 188 us -> 39.5 us
  starting transfers between devices: 93.5 us -> 0 us
  waiting for transfers between devices: 55.5 us -> 0 us
  matrix products: 36.7 us -> 0 us
  between operations: 15.4 us -> 0.64 us
  other arithmetic: 10.7 us -> 1.32 us
  local copies, waits for them, and re-layouts: 0.01 us -> 6.7 us
    pallas_call x0 -> x1, Pallas kernels: none -> 187 us  [on_device(): pl.pallas_call(functools.partial(kernel, n), out_shape=(jax.ShapeDtypeStr...]
    psum x1, blocking collectives: 165 us -> 39.5 us  [on_device(): errors = lax.psum(jnp.sum(part, axis=1), ('blk', 'mp')) / total]
    ppermute x6 -> x0, starting transfers between devices: 93.4 us -> none  [from_behind(): return lax.ppermute(block, axis, route)]
    reduce_scatter x2 -> x0, waiting for transfers between devices: 49.7 us -> none  [gradient(): lax.psum_scatter(partial_value, 'mp', scatter_dimension=1, tiled=True)]
    dot_general x4 -> x0, matrix products: 36.7 us -> none  [the longest x2 26.3 us: gradient(): lax.dot_general(resid, feats, (((0,), (0,)), ((), ())), preferred_element...]
    all_gather x2 -> x0, blocking collectives: 22.7 us -> none  [gradient(): resid = lax.all_gather(resid_local, 'mp', axis=1, tiled=True)]
    unnamed x4 -> x2, local copies, waits for them, and re-layouts: 0.01 us -> 6.7 us
    ppermute x6 -> x0, waiting for transfers between devices: 5.76 us -> none  [from_behind(): return lax.ppermute(block, axis, route)]
  transfers between devices with their start and end apart: 8 -> 0, of which waited for: 4 -> 0; matrix products, arithmetic and copies ran while one was open for 5% -> 0% of each run, Pallas kernels for 0% -> 0%
where the time goes in v1:
time: 235 us
  Pallas kernels  187 us (80%)
  blocking collectives  39.5 us (17%)
  local copies, waits for them, and re-layouts  6.7 us (3%)
    pallas_call x1, Pallas kernels, on_device(): pl.pallas_call(functools.partial(kernel, n), out_shape=(jax.ShapeDtypeStr...  187 us
    psum x1, blocking collectives, on_device(): errors = lax.psum(jnp.sum(part, axis=1), ('blk', 'mp')) / total  39.5 us
    unnamed x2, local copies, waits for them, and re-layouts  6.7 us

profile of v1, /device:TPU:0, one launch (start us, length us, event | category | flops | bytes accessed | tf_op | source)
XLA Modules:
  0.0 235.1 jit_solution(10652076775413043884)
XLA Ops:
  0.6 1.9 copy.5
  2.5 186.9 %shard_map.50 = (bf16[1024,2048]{1,0:T(8,128)(2,1)}, f32[2,512]{1,0:T(2,128)}) custom-call(bf16[1024,2048]{1,0:T(8,128)(2,1)} %bitcast.6, bf16[384,2048]{1,0:T(8,128)(2,1)} %bitcast.9, bf16[512,384]{1,0:T(8,128)(2,1)} %bitcast.8), custom_call_target="tpu_custom_call" | custom-call | tf_op jit(solution)/shard_map/pallas_call | solution.py:194
  189.5 0.8 reduce_sum.9
  190.3 39.5 %psum.7 = f32[2]{0:T(128)S(1)} all-reduce(f32[2]{0:T(128)S(1)} %reduce_sum.9), channel_id=1, replica_groups=mesh['blk'=16,'mp'=2] {'blk','mp'}, use_global_device_ids=true, to_apply=%region_1.0 | all-reduce | flops 2 | bytes 16 | tf_op jit(solution)/shard_map/psum | solution.py:216
  229.8 0.5 broadcast_multiply_fusion
  230.3 4.8 %copy.7 = bf16[1,1024,2048]{2,1,0:T(8,128)(2,1)} copy(bf16[1,1024,2048]{2,1,0:T(8,128)(2,1)} %bitcast.7) | data formatting | bytes 8388608

commit v2 on v1

v2 whole, which is shorter than its diff:
```python
import functools

import jax
import jax.numpy as jnp
from jax import lax
from jax.experimental import pallas as pl
from jax.experimental.pallas import tpu as pltpu
from jax.sharding import PartitionSpec as P

MESH = pl.DeviceIdType.MESH
CHUNKS = 8
COLS = 4
GROUP = 8
FINALS = 5
mix_third = 1.0 / 3.0
step_size = 0.1
F32 = jnp.float32
BF16 = jnp.bfloat16


def dot_nt(a, b):
    return lax.dot_general(a, b, (((1,), (1,)), ((), ())), preferred_element_type=F32)


def dot_nn(a, b):
    return lax.dot_general(a, b, (((1,), (0,)), ((), ())), preferred_element_type=F32)


def kernel(n, total, x, h, t, out, err, xo, far, near, hn, rt, rt2, rn, ps, pr, acc, red_a, red_b, sems, one, asem, bsem, osem):
    d, wide = x.shape
    tokens = h.shape[0]
    half = t.shape[1]
    rows = d // CHUNKS
    cw = wide // COLS
    zs = n // 4
    me = lax.axis_index("blk")
    mp = lax.axis_index("mp")
    core = lax.rem(me, 2)
    par = lax.rem(me // 2, 2)
    low = lax.rem(me, 4)
    z = me // 4
    spot = low * 2 + mp
    sib = me + 1 - 2 * core
    partner = me + 2 - 4 * par
    fwd_to = lax.rem(me + n + 4 - 8 * par, n)
    cross = lax.rem(me + n + 2 * core - 1, n)

    def in_group(o):
        there = lax.rem(spot + o, GROUP)
        return there, (z * 4 + there // 2, lax.rem(there, 2))

    def over_groups(o):
        there = lax.rem(z + o, zs)
        return there, (there * 4 + low, mp)

    barrier = pltpu.get_barrier_semaphore()
    for o in range(1, GROUP):
        pl.semaphore_signal(barrier, inc=1, device_id=in_group(o)[1], device_id_type=MESH)
    for o in range(1, zs):
        pl.semaphore_signal(barrier, inc=1, device_id=over_groups(o)[1], device_id_type=MESH)
    pl.semaphore_signal(barrier, inc=1, device_id=(cross, mp), device_id_type=MESH)
    pl.semaphore_wait(barrier, GROUP + zs - 1)

    def rs(k):
        return pl.ds(k * rows, rows)

    def remote(src, dst, send, recv, dev):
        return pltpu.make_async_remote_copy(
            src_ref=src, dst_ref=dst, send_sem=send, recv_sem=recv, device_id=dev, device_id_type=MESH)

    def copy(src, dst, kind, k, dev):
        return remote(src, dst, sems.at[0, kind, k], sems.at[1, kind, k], dev)

    def c_own(k):
        return copy(x.at[rs(k)], far.at[par, rs(k)], 0, k, (partner, mp))

    def c_fwd(k):
        return copy(far.at[1 - par, rs(k)], far.at[par, rs(k)], 1, k, (fwd_to, mp))

    def c_cross(k):
        return copy(far.at[1 - core, rs(k)], near.at[1 - core, rs(k)], 2, k, (sib, mp))

    def c_rsib(k):
        return copy(rt.at[rs(k)], rn.at[core, rs(k)], 3, k, (sib, mp))

    def mine(k):
        return pl.ds(pl.multiple_of(mp * half + k * rows, rows), rows)

    def c_rcross(k):
        return copy(rt.at[mine(k)], rn.at[1 - core, mine(k)], 4, k, (cross, mp))

    def c_rmp(k):
        return copy(rn.at[core, mine(k)], rn.at[core, mine(k)], 8, k, (me, 1 - mp))

    def c_part(it, k):
        return copy(ps.at[it, rs(k)], pr.at[it, rs(k)], 5 + it, k, (me, 1 - mp))

    def c_hcross(j):
        cs = pl.ds(j * cw, cw)
        return copy(h.at[:, cs], hn.at[1 - core, :, cs], 7, j, (cross, mp))

    def c_out(k):
        return pltpu.make_async_copy(xo.at[rs(k)], out.at[rs(k)], osem.at[k])

    def c_group(o):
        there, dev = in_group(o)
        return remote(red_a.at[spot], red_a.at[spot], asem.at[0, o], asem.at[1, spot], dev)

    def from_group(o):
        there, dev = in_group(o)
        return remote(red_a.at[there], red_a.at[there], asem.at[0, o], asem.at[1, there], dev)

    def c_over(o):
        there, dev = over_groups(o)
        return remote(red_b.at[z], red_b.at[z], bsem.at[0, o], bsem.at[1, z], dev)

    def from_over(o):
        there, dev = over_groups(o)
        return remote(red_b.at[there], red_b.at[there], bsem.at[0, o], bsem.at[1, there], dev)

    c_sib = remote(x, near.at[core], one.at[0, 0], one.at[1, 0], (sib, mp))
    c_hsib = remote(h, hn.at[core], one.at[0, 1], one.at[1, 1], (sib, mp))

    def send_part(it, k, value):
        first = k * rows
        here = mp == first // half
        targ = t[:, pl.ds(first % half, rows)].astype(F32).T
        ps[it, rs(k), :] = (value - jnp.where(here, targ, 0.0)).astype(BF16)
        c_part(it, k).start()

    def take_part(it, k, dst):
        c_part(it, k).wait_recv()
        dst[rs(k), :] = (ps[it, rs(k), :].astype(F32) + pr[it, rs(k), :].astype(F32)).astype(BF16)

    def add_err(row, diff):
        v = jnp.sum(diff * diff, axis=0, keepdims=True)
        acc[row:row + 1, :] += sum(v[:, q:q + 128] for q in range(0, cw, 128))

    def columns(j):
        return pl.ds(pl.multiple_of(j * cw, cw), cw)

    def neighbour(r, cs, side):
        track = (dot_nn(rn[side, r, :], hn[side, :, cs]) / tokens).astype(BF16).astype(F32)
        own, there, beyond = x[r, cs].astype(F32), near[side, r, cs].astype(F32), far[side, r, cs].astype(F32)
        state = (own + there + beyond) * mix_third - step_size * track
        return track, state.astype(BF16).astype(F32)

    def err_pass(k):
        def body(j, _):
            cs = columns(j)
            add_err(1, xo[rs(k), cs].astype(F32) - neighbour(rs(k), cs, 1)[1])
            return 0
        lax.fori_loop(0, COLS, body, 0)

    def last_step(k, with_err):
        r = rs(k)

        def body(j, _):
            cs = columns(j)
            older = dot_nn(rt[r, :], h[:, cs]) / tokens
            fresh = dot_nn(rt2[r, :], h[:, cs]) / tokens
            below, x_lo = neighbour(r, cs, 0)
            above, x_hi = neighbour(r, cs, 1)
            track = older.astype(BF16).astype(F32)
            track = ((below + track + above) * mix_third + fresh - older).astype(BF16).astype(F32)
            x_me = xo[r, cs].astype(F32)
            if with_err:
                add_err(1, x_me - x_hi)
            xo[r, cs] = ((x_lo + x_me + x_hi) * mix_third - step_size * track).astype(BF16)
            return 0

        lax.fori_loop(0, COLS, body, 0)
        c_out(k).start()

    def middle_step(k):
        def body(j, _):
            cs = columns(j)
            track = (dot_nn(rt[rs(k), :], h[:, cs]) / tokens).astype(BF16)
            own = x[rs(k), cs].astype(F32)
            above = near[1, rs(k), cs].astype(F32)
            add_err(0, own - above)
            blend = (near[0, rs(k), cs].astype(F32) + own + above) * mix_third
            xo[rs(k), cs] = (blend - step_size * track.astype(F32)).astype(BF16)
            return 0

        lax.fori_loop(0, COLS, body, 0)
        send_part(1, k, dot_nt(xo[rs(k), :], h[...]))

    early = 2
    halves = half // rows
    for k in range(early):
        c_own(k).start()
    c_sib.start()
    c_hsib.start()
    acc[...] = jnp.zeros_like(acc)
    for k in range(CHUNKS):
        send_part(0, k, dot_nt(x[rs(k), :], h[...]))
    for k in range(CHUNKS):
        take_part(0, k, rt)
    for k in range(halves):
        c_rcross(k).start()
    for k in range(CHUNKS):
        c_rsib(k).start()
    for j in range(COLS):
        c_hcross(j).start()
    c_sib.wait_recv()

    ready = FINALS
    done = 0
    for s in range(CHUNKS + 3):
        if s == ready:
            for k in range(halves):
                c_rcross(k).wait_recv()
                c_rmp(k).start()
            c_hsib.wait_recv()
            for k in range(CHUNKS):
                c_rsib(k).wait_recv()
            for j in range(COLS):
                c_hcross(j).wait_recv()
            for k in range(halves):
                c_rmp(k).wait_recv()
        if 0 <= s - 2 < CHUNKS:
            c_cross(s - 2).wait_recv()
            middle_step(s - 2)
        if 0 <= s - 1 < CHUNKS:
            c_fwd(s - 1).wait_recv()
            c_cross(s - 1).start()
        if s < CHUNKS:
            c_own(s).wait_recv()
            c_fwd(s).start()
            if s + early < CHUNKS:
                c_own(s + early).start()
        if s - 3 == CHUNKS - 1:
            err_pass(CHUNKS - 1)
            red_a[spot] = acc[...]
            for o in range(1, GROUP):
                c_group(o).start()
        if 0 <= s - 3 < CHUNKS:
            take_part(1, s - 3, rt2)
        if s >= ready:
            for k in range(done, min(s - 2, done + 2, CHUNKS)):
                last_step(k, k < CHUNKS - 1)
                done = k + 1

    for k in range(done, CHUNKS):
        last_step(k, k < CHUNKS - 1)
    for o in range(1, GROUP):
        from_group(o).wait_recv()
    value = red_a[0]
    for o in range(1, GROUP):
        value += red_a[o]
    red_b[z] = value
    for o in range(1, zs):
        c_over(o).start()
    c_sib.wait_send()
    c_hsib.wait_send()
    for k in range(CHUNKS):
        for c in (c_own(k), c_fwd(k), c_cross(k), c_rsib(k), c_part(0, k), c_part(1, k)):
            c.wait_send()
        c_out(k).wait()
    for k in range(halves):
        c_rcross(k).wait_send()
        c_rmp(k).wait_send()
    for j in range(COLS):
        c_hcross(j).wait_send()
    for o in range(1, GROUP):
        c_group(o).wait_send()
    for o in range(1, zs):
        from_over(o).wait_recv()
    value = red_b[0]
    for o in range(1, zs):
        value += red_b[o]
    for o in range(1, zs):
        c_over(o).wait_send()
    for row in range(2):
        err[row] = jnp.sum(value[row:row + 1, :]) / total


def solution(mesh):
    n = mesh.shape["blk"]

    def on_device(params, hidden, targets):
        x, h, t = params[0], hidden[0], targets[0]
        d, wide = x.shape
        tokens = h.shape[0]
        total = float(wide * mesh.shape["mp"] * n)
        vmem = pl.BlockSpec(memory_space=pltpu.VMEM)
        dma = pltpu.SemaphoreType.DMA
        new, errors = pl.pallas_call(
            functools.partial(kernel, n, total),
            out_shape=(jax.ShapeDtypeStruct((d, wide), BF16), jax.ShapeDtypeStruct((2,), F32)),
            in_specs=[vmem] * 3,
            out_specs=(pl.BlockSpec(memory_space=pl.ANY), pl.BlockSpec(memory_space=pltpu.SMEM)),
            scratch_shapes=[
                pltpu.VMEM((d, wide), BF16),
                pltpu.VMEM((2, d, wide), BF16),
                pltpu.VMEM((2, d, wide), BF16),
                pltpu.VMEM((2, tokens, wide), BF16),
                pltpu.VMEM((d, tokens), BF16),
                pltpu.VMEM((d, tokens), BF16),
                pltpu.VMEM((2, d, tokens), BF16),
                pltpu.VMEM((2, d, tokens), BF16),
                pltpu.VMEM((2, d, tokens), BF16),
                pltpu.VMEM((8, 128), F32),
                pltpu.VMEM((GROUP, 8, 128), F32),
                pltpu.VMEM((n // 4, 8, 128), F32),
                dma((2, 9, max(CHUNKS, COLS))),
                dma((2, 2)),
                dma((2, GROUP)),
                dma((2, n // 4)),
                dma((CHUNKS,)),
            ],
            compiler_params=pltpu.CompilerParams(
                collective_id=0, has_side_effects=True, vmem_limit_bytes=60 * 1024 * 1024),
        )(x, h, t)
        return new[None], errors

    placed = (P("blk", None, "mp"),) * 3
    return jax.shard_map(
        on_device, mesh=mesh, in_specs=placed,
        out_specs=(P("blk", None, "mp"), P()), check_vma=False)
```

time: 235 us -> 179 us (0.76)
  blocking collectives: 39.5 us -> 0 us
  Pallas kernels: 187 us -> 172 us
    psum x1 -> x0, blocking collectives: 39.5 us -> none  [on_device(): errors = lax.psum(jnp.sum(part, axis=1), ('blk', 'mp')) / total]
    pallas_call x1, Pallas kernels: 187 us -> 172 us  [on_device(): pl.pallas_call(functools.partial(kernel, n, total), out_shape=(jax.ShapeD...]
    unnamed x2 -> x4, local copies, waits for them, and re-layouts: 6.7 us -> 5.3 us
where the time goes in v2:
time: 179 us; the launch traced here: 178 us
  Pallas kernels  172 us (96%)
  local copies, waits for them, and re-layouts  5.3 us (3%)
    pallas_call x1, Pallas kernels, on_device(): pl.pallas_call(functools.partial(kernel, n, total), out_shape=(jax.ShapeD...  172 us
    unnamed x4, local copies, waits for them, and re-layouts  5.3 us

profile of v2, /device:TPU:0, one launch (start us, length us, event | category | flops | bytes accessed | tf_op | source)
XLA Modules:
  0.0 178.4 jit_solution(1886912920343782575)
XLA Ops:
  0.6 172.5 %shard_map.50 = (bf16[1024,2048]{1,0:T(8,128)(2,1)}, f32[2]{0:T(128)}) custom-call(bf16[1024,2048]{1,0:T(8,128)(2,1)} %bitcast.4, bf16[384,2048]{1,0:T(8,128)(2,1)} %bitcast.6, bf16[384,512]{1,0:T(8,128)(2,1)} %bitcast.7), custom_call_target="tpu_custom_call" | custom-call | tf_op jit(solution)/shard_map/pallas_call | solution.py:289
  173.1 0.0 copy-start
  173.1 4.8 %copy.7 = bf16[1,1024,2048]{2,1,0:T(8,128)(2,1)} copy(bf16[1,1024,2048]{2,1,0:T(8,128)(2,1)} %bitcast.5) | data formatting | bytes 8388608
  177.9 0.0 copy-done
  177.9 0.5 copy.8
Async XLA Ops:
  173.1 4.8 %copy-start = (f32[2]{0:T(128)S(1)}, f32[2]{0:T(128)}, u32[]{:S(2)}) copy-start(f32[2]{0:T(128)} %get-tuple-element.9) | copy-start | bytes 28

commit v3 on v2

--- a/solution.py
+++ b/solution.py
@@ -8,7 +8,9 @@
 from jax.sharding import PartitionSpec as P
 
 MESH = pl.DeviceIdType.MESH
-CHUNKS = 8
+PARTS = 8
+SIZES = (2, 2, 2, 2, 2, 2, 1, 1, 1, 1)
+CHUNKS = len(SIZES)
 COLS = 4
 GROUP = 8
 FINALS = 5
@@ -26,11 +28,12 @@
     return lax.dot_general(a, b, (((1,), (0,)), ((), ())), preferred_element_type=F32)
 
 
-def kernel(n, total, x, h, t, out, err, xo, far, near, hn, rt, rt2, rn, ps, pr, acc, red_a, red_b, sems, one, asem, bsem, osem):
+def kernel(n, total, x, h, t, xo, err, far, near, hn, rt, rt2, rn, ps, pr, acc, red_a, red_b, sems, one, asem, bsem):
     d, wide = x.shape
     tokens = h.shape[0]
     half = t.shape[1]
-    rows = d // CHUNKS
+    rows = d // PARTS
+    unit = d // sum(SIZES)
     cw = wide // COLS
     zs = n // 4
     me = lax.axis_index("blk")
@@ -62,7 +65,7 @@
     pl.semaphore_wait(barrier, GROUP + zs - 1)
 
     def rs(k):
-        return pl.ds(k * rows, rows)
+        return pl.ds(sum(SIZES[:k]) * unit, SIZES[k] * unit)
 
     def remote(src, dst, send, recv, dev):
         return pltpu.make_async_remote_copy(
@@ -99,9 +102,6 @@
         cs = pl.ds(j * cw, cw)
         return copy(h.at[:, cs], hn.at[1 - core, :, cs], 7, j, (cross, mp))
 
-    def c_out(k):
-        return pltpu.make_async_copy(xo.at[rs(k)], out.at[rs(k)], osem.at[k])
-
     def c_group(o):
         there, dev = in_group(o)
         return remote(red_a.at[spot], red_a.at[spot], asem.at[0, o], asem.at[1, spot], dev)
@@ -122,9 +122,9 @@
     c_hsib = remote(h, hn.at[core], one.at[0, 1], one.at[1, 1], (sib, mp))
 
     def send_part(it, k, value):
-        first = k * rows
+        first = sum(SIZES[:k]) * unit
         here = mp == first // half
-        targ = t[:, pl.ds(first % half, rows)].astype(F32).T
+        targ = t[:, pl.ds(first % half, SIZES[k] * unit)].astype(F32).T
         ps[it, rs(k), :] = (value - jnp.where(here, targ, 0.0)).astype(BF16)
         c_part(it, k).start()
 
@@ -170,7 +170,6 @@
             return 0
 
         lax.fori_loop(0, COLS, body, 0)
-        c_out(k).start()
 
     def middle_step(k):
         def body(j, _):
@@ -186,7 +185,8 @@
         lax.fori_loop(0, COLS, body, 0)
         send_part(1, k, dot_nt(xo[rs(k), :], h[...]))
 
-    early = 2
+    early = 3
+    last = CHUNKS - 1
     halves = half // rows
     for k in range(early):
         c_own(k).start()
@@ -219,6 +219,8 @@
                 c_hcross(j).wait_recv()
             for k in range(halves):
                 c_rmp(k).wait_recv()
+        if s - 2 == last:
+            err_pass(last - 1)
         if 0 <= s - 2 < CHUNKS:
             c_cross(s - 2).wait_recv()
             middle_step(s - 2)
@@ -230,34 +232,32 @@
             c_fwd(s).start()
             if s + early < CHUNKS:
                 c_own(s + early).start()
-        if s - 3 == CHUNKS - 1:
-            err_pass(CHUNKS - 1)
+        if s - 2 == last:
+            err_pass(last)
             red_a[spot] = acc[...]
             for o in range(1, GROUP):
                 c_group(o).start()
+        if s - 3 == last:
+            for o in range(1, GROUP):
+                from_group(o).wait_recv()
+            value = red_a[0]
+            for o in range(1, GROUP):
+                value += red_a[o]
+            red_b[z] = value
+            for o in range(1, zs):
+                c_over(o).start()
         if 0 <= s - 3 < CHUNKS:
             take_part(1, s - 3, rt2)
         if s >= ready:
             for k in range(done, min(s - 2, done + 2, CHUNKS)):
-                last_step(k, k < CHUNKS - 1)
+                last_step(k, k < last - 1)
                 done = k + 1
 
-    for k in range(done, CHUNKS):
-        last_step(k, k < CHUNKS - 1)
-    for o in range(1, GROUP):
-        from_group(o).wait_recv()
-    value = red_a[0]
-    for o in range(1, GROUP):
-        value += red_a[o]
-    red_b[z] = value
-    for o in range(1, zs):
-        c_over(o).start()
     c_sib.wait_send()
     c_hsib.wait_send()
     for k in range(CHUNKS):
         for c in (c_own(k), c_fwd(k), c_cross(k), c_rsib(k), c_part(0, k), c_part(1, k)):
             c.wait_send()
-        c_out(k).wait()
     for k in range(halves):
         c_rcross(k).wait_send()
         c_rmp(k).wait_send()
@@ -288,11 +288,10 @@
         dma = pltpu.SemaphoreType.DMA
         new, errors = pl.pallas_call(
             functools.partial(kernel, n, total),
-            out_shape=(jax.ShapeDtypeStruct((d, wide), BF16), jax.ShapeDtypeStruct((2,), F32)),
+            out_shape=(pltpu.VMEM((d, wide), BF16), jax.ShapeDtypeStruct((2,), F32)),
             in_specs=[vmem] * 3,
-            out_specs=(pl.BlockSpec(memory_space=pl.ANY), pl.BlockSpec(memory_space=pltpu.SMEM)),
+            out_specs=(vmem, pl.BlockSpec(memory_space=pltpu.SMEM)),
             scratch_shapes=[
-                pltpu.VMEM((d, wide), BF16),
                 pltpu.VMEM((2, d, wide), BF16),
                 pltpu.VMEM((2, d, wide), BF16),
                 pltpu.VMEM((2, tokens, wide), BF16),
@@ -308,10 +307,9 @@
                 dma((2, 2)),
                 dma((2, GROUP)),
                 dma((2, n // 4)),
-                dma((CHUNKS,)),
             ],
             compiler_params=pltpu.CompilerParams(
-                collective_id=0, has_side_effects=True, vmem_limit_bytes=60 * 1024 * 1024),
+                collective_id=0, has_side_effects=True, vmem_limit_bytes=48 * 1024 * 1024),
         )(x, h, t)
         return new[None], errors
 

time: 179 us -> 183 us (1.022)
  Pallas kernels: 172 us -> 178 us
    pallas_call x1, Pallas kernels: 172 us -> 178 us  [on_device(): pl.pallas_call(functools.partial(kernel, n, total), out_shape=(pltpu.VMEM...]
    unnamed x4 -> x6, local copies, waits for them, and re-layouts: 5.3 us -> 4.92 us
where the time goes in v3:
time: 183 us
  Pallas kernels  178 us (97%)
  local copies, waits for them, and re-layouts  4.92 us (3%)
    pallas_call x1, Pallas kernels, on_device(): pl.pallas_call(functools.partial(kernel, n, total), out_shape=(pltpu.VMEM...  178 us
    unnamed x6, local copies, waits for them, and re-layouts  4.92 us

profile of v3, /device:TPU:0, one launch (start us, length us, event | category | flops | bytes accessed | tf_op | source)
XLA Modules:
  0.0 183.2 jit_solution(1968989988794754727)
XLA Ops:
  0.6 0.0 copy-start
  0.6 1.4 copy-done
  2.0 0.0 copy-start.1
  2.0 1.0 copy-done.1
  3.0 177.6 %shard_map.50 = (bf16[1024,2048]{1,0:T(8,128)(2,1)S(1)}, f32[2]{0:T(128)S(1)}) custom-call(bf16[1024,2048]{1,0:T(8,128)(2,1)} %bitcast.7, bf16[384,2048]{1,0:T(8,128)(2,1)S(1)} %bitcast.5, bf16[384,512]{1,0:T(8,128)(2,1)S(1)} %bitcast.6), custom_call_target="tpu_custom_call" | custom-call | tf_op jit(solution)/shard_map/pallas_call | solution.py:289
  180.7 2.0 %copy.7 = bf16[1,1024,2048]{2,1,0:T(8,128)(2,1)} copy(bf16[1,1024,2048]{2,1,0:T(8,128)(2,1)S(1)} %bitcast.4) | data formatting | bytes 8388608
  182.7 0.5 copy.8
Async XLA Ops:
  0.6 1.4 copy-start
  2.0 1.0 copy-start.1

commit v4 on v3

--- a/solution.py
+++ b/solution.py
@@ -9,7 +9,7 @@
 
 MESH = pl.DeviceIdType.MESH
 PARTS = 8
-SIZES = (2, 2, 2, 2, 2, 2, 1, 1, 1, 1)
+SIZES = (2,) * 8
 CHUNKS = len(SIZES)
 COLS = 4
 GROUP = 8
@@ -185,7 +185,7 @@
         lax.fori_loop(0, COLS, body, 0)
         send_part(1, k, dot_nt(xo[rs(k), :], h[...]))
 
-    early = 3
+    early = 2
     last = CHUNKS - 1
     halves = half // rows
     for k in range(early):

time: 183 us -> 176 us (0.962)
  Pallas kernels: 178 us -> 171 us
    pallas_call x1, Pallas kernels: 178 us -> 171 us  [on_device(): pl.pallas_call(functools.partial(kernel, n, total), out_shape=(pltpu.VMEM...]
where the time goes in v4:
time: 176 us
  Pallas kernels  171 us (97%)
  local copies, waits for them, and re-layouts  4.92 us (3%)
    pallas_call x1, Pallas kernels, on_device(): pl.pallas_call(functools.partial(kernel, n, total), out_shape=(pltpu.VMEM...  171 us
    unnamed x6, local copies, waits for them, and re-layouts  4.92 us

profile of v4, /device:TPU:0, one launch (start us, length us, event | category | flops | bytes accessed | tf_op | source)
XLA Modules:
  0.0 176.1 jit_solution(16831455337473435788)
XLA Ops:
  0.6 0.0 copy-start
  0.6 1.4 copy-done
  2.0 0.0 copy-start.1
  2.0 1.0 copy-done.1
  3.0 170.5 %shard_map.50 = (bf16[1024,2048]{1,0:T(8,128)(2,1)S(1)}, f32[2]{0:T(128)S(1)}) custom-call(bf16[1024,2048]{1,0:T(8,128)(2,1)} %bitcast.7, bf16[384,2048]{1,0:T(8,128)(2,1)S(1)} %bitcast.5, bf16[384,512]{1,0:T(8,128)(2,1)S(1)} %bitcast.6), custom_call_target="tpu_custom_call" | custom-call | tf_op jit(solution)/shard_map/pallas_call | solution.py:289
  173.6 2.0 %copy.7 = bf16[1,1024,2048]{2,1,0:T(8,128)(2,1)} copy(bf16[1,1024,2048]{2,1,0:T(8,128)(2,1)S(1)} %bitcast.4) | data formatting | bytes 8388608
  175.6 0.5 copy.8
Async XLA Ops:
  0.6 1.4 copy-start
  2.0 1.0 copy-start.1
